TPU v7x, 32 devices: a whole 2x2x4 slice. The times are simulated.
32 devices in a mesh: row: 8 (over z, x), col: 4 (over y, core).
Axes of the slice: x: 2, y: 2, z: 4, core: 2. Of those that a mesh axis runs over, the one named last changes fastest.
Arguments:
- forward_map: float32 [2048, 16384], P('row', 'col'), may hold values from -0.125 to 0.125
- sensor_weights: float32 [2048], P('row'), may hold values from 0.25 to 4
- sensor_mask: int32 [2048], P('row'), may hold values 0 or 1
Outputs:
- gram_matrix: float32 [16384, 16384], P('row', 'col')
All inputs are finite; a program needn't handle non-finite values. No bound on the sum of `sensor_mask` on one device may be relied on, other than what follows from the above.
Results may differ from a plain program's by a relative error of at most 0.000061.
Values sent between devices are 32-bit elements; how exact they have to be, the bound alone decides.
No kernel may reach another device: no remote copies, remote signals or barrier semaphores. Data moves between devices by JAX's collectives and lax.ppermute only.
A program may use at most 128 MiB of HBM per device.

v0:
```python
import jax
import jax.numpy as jnp
from jax import lax
from jax.sharding import PartitionSpec as P


def contract(left_rows, right_rows):
    return lax.dot_general(
        left_rows,
        right_rows,
        (((0,), (0,)), ((), ())),
        precision=lax.Precision.HIGHEST,
        preferred_element_type=jnp.float32,
    )


def per_device(forward_map, sensor_weights, sensor_mask):
    sensor_scale = sensor_weights * sensor_mask.astype(jnp.float32)
    weighted = forward_map * sensor_scale[:, None]
    gathered = lax.all_gather(weighted, "row", axis=0, tiled=True)
    spread = lax.all_to_all(forward_map, "col", split_axis=0, concat_axis=1, tiled=True)
    regrouped = lax.all_to_all(spread, "row", split_axis=1, concat_axis=0, tiled=True)
    rows_count = lax.axis_size("row")
    cols_count = lax.axis_size("col")
    columns = gathered.shape[1]
    stride_rows = gathered.shape[0] // (rows_count * cols_count)
    permuted = (
        gathered.reshape(rows_count, cols_count, stride_rows, columns)
        .transpose(1, 0, 2, 3)
        .reshape(-1, columns)
    )
    return contract(lax.all_gather(regrouped, "col", axis=0, tiled=True), permuted)


def solution(mesh):
    placed = (P("row", "col"), P("row"), P("row"))
    return jax.shard_map(
        per_device, mesh=mesh, in_specs=placed, out_specs=P("row", "col"), check_vma=False
    )
```

profile of v0, /device:TPU:0, one launch (start us, length us, event | category | flops | bytes accessed | tf_op | source)
XLA Modules:
  0.0 1065.3 jit_solution(8509121159541855739)
XLA Ops:
  6.5 0.0 all-gather.3.cloned.1.call-start
  6.5 0.7 convert_multiply_fusion
  7.2 4.8 broadcast_multiply_fusion
  12.0 0.0 all-gather.3.cloned.1.call-update
  12.0 0.0 all-gather.5.cloned.1.call-start
  12.1 52.6 %all_to_all.35 = f32[4,64,4096]{2,1,0:T(8,128)S(1)} all-to-all(f32[4,64,4096]{2,1,0:T(8,128)} %bitcast.15), channel_id=1, replica_groups=mesh['row'=8,'col'=4] {'col'}, dimensions={0} | all-to-all | bytes 8388608 | tf_op jit(solution)/shard_map/all_to_all | solution.py:21
  64.7 4.7 copy.13
  69.4 5.5 all_to_all.29
  74.9 4.6 copy.14
  79.5 136.9 %all_to_all.36 = f32[64,8,2048]{2,0,1:T(8,128)} all-to-all(f32[64,8,2048]{2,0,1:T(8,128)S(1)} %copy.14), channel_id=1, replica_groups=mesh['row'=8,'col'=4] {'row'}, dimensions={1} | all-to-all | bytes 8388608 | tf_op jit(solution)/shard_map/all_to_all | solution.py:22
  216.4 0.0 all-gather.5.cloned.1.call-update
  216.4 481.1 %all-gather.3.cloned.1.call-done = f32[2048,4096]{1,0:T(8,128)} async-done(((f32[256,4096]{1,0:T(8,128)}), f32[2048,4096]{1,0:T(8,128)}) %all-gather.3.cloned.1.call-update) | async-done | bytes 33554448 | tf_op jit(solution)/shard_map/all_gather | solution.py:20
  697.5 24.4 %copy.12 = f32[4,8,64,4096]{3,2,1,0:T(8,128)} copy(f32[4,8,64,4096]{3,2,0,1:T(8,128)} %bitcast.13) | data formatting | bytes 67108864 | tf_op jit(solution)/shard_map/transpose | solution.py:29
  721.9 83.1 %all-gather.5.cloned.1.call-done = f32[2048,2048]{1,0:T(8,128)} async-done(((f32[512,2048]{1,0:T(8,128)}), f32[2048,2048]{1,0:T(8,128)}) %all-gather.5.cloned.1.call-update) | async-done | bytes 16777232 | tf_op jit(solution)/shard_map/all_gather | solution.py:32
  805.0 222.4 %convolution_bitcast_fusion = f32[2048,4096]{0,1:T(8,128)} fusion(f32[2048,4096]{1,0:T(8,128)} %bitcast.14, f32[2048,2048]{1,0:T(8,128)} %all-gather.5.cloned.1.call-done), kind=kOutput, calls=%fused_computation | convolution fusion | flops 206158430208 | bytes 83886080 | tf_op jit(solution)/shard_map/dot_general | solution.py:8
  1027.4 31.1 %copy.15 = f32[2048,4096]{1,0:T(8,128)} copy(f32[2048,4096]{0,1:T(8,128)} %convolution_bitcast_fusion) | data formatting | bytes 67108864 | tf_op jit(solution)/shard_map/dot_general | solution.py:8
Async XLA Ops:
  6.5 691.0 %all-gather.3.cloned.1.call-start = ((), (), s32[]{:S(2)}) async-start(), calls=%async_computation.2 | async-start | bytes 37748736 | tf_op jit(solution)/shard_map/all_gather | solution.py:20
  12.0 792.9 %all-gather.5.cloned.1.call-start = ((), (), s32[]{:S(2)}) async-start(), calls=%async_computation.3 | async-start | bytes 20971520 | tf_op jit(solution)/shard_map/all_gather | solution.py:32
Sparse Core Ops, SparseCore 0:
  12.2 685.3 all-gather.2
  699.1 105.8 all-gather.4
where the time goes:
time: 1070 us
  waiting for transfers between devices  564 us (53%)
  matrix products  222 us (21%)
  blocking collectives  189 us (18%)
  local copies, waits for them, and re-layouts  70.2 us (7%)
  between operations  13.4 us (1%)
    all_gather x1, waiting for transfers between devices, per_device(): gathered = lax.all_gather(weighted, 'row', axis=0, tiled=True)  481 us
    dot_general x1, matrix products, contract(): lax.dot_general(left_rows, right_rows, (((0,), (0,)), ((), ())), precisio...  222 us
    all_to_all x1, blocking collectives, per_device(): lax.all_to_all(spread, 'row', split_axis=1, concat_axis=0, tiled=True)  137 us
    all_gather x1, waiting for transfers between devices, per_device(): lax.all_gather(regrouped, 'col', axis=0, tiled=True)  83.1 us
    all_to_all x1, blocking collectives, per_device(): lax.all_to_all(forward_map, 'col', split_axis=0, concat_axis=1, tiled=True)  52.6 us
    dot_general x1, local copies, waits for them, and re-layouts, contract(): lax.dot_general(left_rows, right_rows, (((0,), (0,)), ((), ())), precisio...  31.1 us
    transpose x1, local copies, waits for them, and re-layouts, per_device(): permuted = gathered.reshape(rows_count, cols_count, stride_rows, columns)...  24.4 us
  transfers between devices with their start and end apart: 2, of which 2 were waited for; matrix products, arithmetic and copies ran while one was open for 3% of the time, Pallas kernels for 0%

commit v1 on v0

--- a/solution.py
+++ b/solution.py
@@ -19,7 +19,10 @@
     weighted = forward_map * sensor_scale[:, None]
     gathered = lax.all_gather(weighted, "row", axis=0, tiled=True)
     spread = lax.all_to_all(forward_map, "col", split_axis=0, concat_axis=1, tiled=True)
-    regrouped = lax.all_to_all(spread, "row", split_axis=1, concat_axis=0, tiled=True)
+    regrouped = jnp.concatenate(
+        lax.all_to_all(jnp.stack(jnp.split(spread, lax.axis_size("row"), axis=1)), "row", 0, 0),
+        axis=0,
+    )
     rows_count = lax.axis_size("row")
     cols_count = lax.axis_size("col")
     columns = gathered.shape[1]

time: 1070 us -> 1030 us (0.963)
  local copies, waits for them, and re-layouts: 70.2 us -> 24.9 us
    dot_general x1 -> x0, local copies, waits for them, and re-layouts: 31.1 us -> none  [contract(): lax.dot_general(left_rows, right_rows, (((0,), (0,)), ((), ())), precisio...]
  transfers between devices with their start and end apart: 2 -> 2, of which waited for: 2 -> 2; matrix products, arithmetic and copies ran while one was open for 3% -> 2% of each run, Pallas kernels for 0% -> 0%
where the time goes in v1:
time: 1030 us
  waiting for transfers between devices  571 us (55%)
  matrix products  222 us (22%)
  blocking collectives  197 us (19%)
  local copies, waits for them, and re-layouts  24.9 us (2%)
  between operations  13.5 us (1%)
    all_gather x1, waiting for transfers between devices, per_device(): gathered = lax.all_gather(weighted, 'row', axis=0, tiled=True)  488 us
    dot_general x1, matrix products, contract(): lax.dot_general(left_rows, right_rows, (((0,), (0,)), ((), ())), precisio...  222 us
    all_to_all x1, blocking collectives, per_device(): lax.all_to_all(jnp.stack(jnp.split(spread, lax.axis_size('row'), axis=1))...  144 us
    all_gather x1, waiting for transfers between devices, per_device(): lax.all_gather(regrouped, 'col', axis=0, tiled=True)  83.3 us
    all_to_all x1, blocking collectives, per_device(): lax.all_to_all(forward_map, 'col', split_axis=0, concat_axis=1, tiled=True)  52.6 us
    transpose x1, local copies, waits for them, and re-layouts, per_device(): permuted = gathered.reshape(rows_count, cols_count, stride_rows, columns)...  24.2 us
  transfers between devices with their start and end apart: 2, of which 2 were waited for; matrix products, arithmetic and copies ran while one was open for 2% of the time, Pallas kernels for 0%

profile of v1, /device:TPU:0, one launch (start us, length us, event | category | flops | bytes accessed | tf_op | source)
XLA Modules:
  0.0 1034.2 jit_solution(4547697736424987361)
XLA Ops:
  6.5 0.0 all-gather.5.cloned.1.call-start
  6.5 0.7 convert_multiply_fusion
  7.2 4.8 broadcast_multiply_fusion
  12.0 0.0 all-gather.5.cloned.1.call-update
  12.0 0.0 all-gather.3.cloned.1.call-start
  12.1 52.6 %all_to_all.24 = f32[4,64,4096]{2,1,0:T(8,128)S(1)} all-to-all(f32[4,64,4096]{2,1,0:T(8,128)} %bitcast.53), channel_id=1, replica_groups=mesh['row'=8,'col'=4] {'col'}, dimensions={0} | all-to-all | bytes 8388608 | tf_op jit(solution)/shard_map/all_to_all | solution.py:21
  64.7 0.4 copy.9
  65.5 144.5 %all_to_all.25 = f32[8,64,2048]{2,1,0:T(8,128)} all-to-all(f32[8,64,2048]{2,1,0:T(8,128)S(1)} %fusion), channel_id=1, replica_groups=mesh['row'=8,'col'=4] {'row'}, dimensions={0} | all-to-all | bytes 8388608 | tf_op jit(solution)/shard_map/all_to_all | solution.py:23
  210.0 0.0 all-gather.3.cloned.1.call-update
  210.0 487.5 %all-gather.5.cloned.1.call-done = f32[2048,4096]{1,0:T(8,128)} async-done(((f32[256,4096]{1,0:T(8,128)}), f32[2048,4096]{1,0:T(8,128)}) %all-gather.5.cloned.1.call-update) | async-done | bytes 33554448 | tf_op jit(solution)/shard_map/all_gather | solution.py:20
  697.5 24.2 %copy.8 = f32[4,8,64,4096]{3,2,1,0:T(8,128)} copy(f32[4,8,64,4096]{3,2,0,1:T(8,128)} %bitcast.43) | data formatting | bytes 67108864 | tf_op jit(solution)/shard_map/transpose | solution.py:32
  721.7 83.3 %all-gather.3.cloned.1.call-done = f32[2048,2048]{1,0:T(8,128)} async-done(((f32[512,2048]{1,0:T(8,128)}), f32[2048,2048]{1,0:T(8,128)}) %all-gather.3.cloned.1.call-update) | async-done | bytes 16777232 | tf_op jit(solution)/shard_map/all_gather | solution.py:35
  805.0 222.3 %fusion.8 = f32[2048,4096]{1,0:T(8,128)} fusion(f32[2048,2048]{1,0:T(8,128)} %all-gather.3.cloned.1.call-done, f32[2048,4096]{1,0:T(8,128)} %bitcast.44), kind=kOutput, calls=%fused_computation.18 | convolution fusion | flops 206158430208 | bytes 83886080 | tf_op jit(solution)/shard_map/dot_general | solution.py:8
  (8 shorter events, 0.3 us)
Async XLA Ops:
  6.5 691.0 %all-gather.5.cloned.1.call-start = ((), (), s32[]{:S(2)}) async-start(), calls=%async_computation.3 | async-start | bytes 37748736 | tf_op jit(solution)/shard_map/all_gather | solution.py:20
  12.0 792.9 %all-gather.3.cloned.1.call-start = ((), (), s32[]{:S(2)}) async-start(), calls=%async_computation.2 | async-start | bytes 20971520 | tf_op jit(solution)/shard_map/all_gather | solution.py:35
Sparse Core Ops, SparseCore 0:
  12.2 685.3 all-gather.4
  699.1 105.8 all-gather.2

commit v2 on v0

--- a/solution.py
+++ b/solution.py
@@ -29,7 +29,12 @@
         .transpose(1, 0, 2, 3)
         .reshape(-1, columns)
     )
-    return contract(lax.all_gather(regrouped, "col", axis=0, tiled=True), permuted)
+    return contract(
+        jnp.concatenate(
+            lax.all_to_all(jnp.stack([regrouped] * lax.axis_size("col")), "col", 0, 0), axis=0
+        ),
+        permuted,
+    )
 
 
 def solution(mesh):

time: 1070 us -> 982 us (0.918)
  waiting for transfers between devices: 564 us -> 466 us
    all_gather x1 -> x0, waiting for transfers between devices: 83.1 us -> none  [per_device(): lax.all_gather(regrouped, 'col', axis=0, tiled=True)]
    all_gather x1, waiting for transfers between devices: 481 us -> 466 us  [per_device(): gathered = lax.all_gather(weighted, 'row', axis=0, tiled=True)]
  transfers between devices with their start and end apart: 2 -> 2, of which waited for: 2 -> 1; matrix products, arithmetic and copies ran while one was open for 3% -> 4% of each run, Pallas kernels for 0% -> 0%
where the time goes in v2:
time: 982 us; the launch traced here: 981 us
  waiting for transfers between devices  466 us (47%)
  matrix products  222 us (23%)
  blocking collectives  189 us (19%)
  local copies, waits for them, and re-layouts  77.3 us (8%)
  between operations  13.4 us (1%)
    all_gather x1, waiting for transfers between devices, per_device(): gathered = lax.all_gather(weighted, 'row', axis=0, tiled=True)  466 us
    dot_general x1, matrix products, contract(): lax.dot_general(left_rows, right_rows, (((0,), (0,)), ((), ())), precisio...  222 us
    all_to_all x1, blocking collectives, per_device(): lax.all_to_all(spread, 'row', split_axis=1, concat_axis=0, tiled=True)  137 us
    all_to_all x1, blocking collectives, per_device(): lax.all_to_all(forward_map, 'col', split_axis=0, concat_axis=1, tiled=True)  52.6 us
    dot_general x1, local copies, waits for them, and re-layouts, contract(): lax.dot_general(left_rows, right_rows, (((0,), (0,)), ((), ())), precisio...  31.1 us
    transpose x1, local copies, waits for them, and re-layouts, per_device(): permuted = gathered.reshape(rows_count, cols_count, stride_rows, columns)...  23.1 us
  transfers between devices with their start and end apart: 2, of which 1 were waited for; matrix products, arithmetic and copies ran while one was open for 4% of the time, Pallas kernels for 0%

profile of v2, /device:TPU:0, one launch (start us, length us, event | category | flops | bytes accessed | tf_op | source)
XLA Modules:
  0.0 980.9 jit_solution(14842906037720717389)
XLA Ops:
  6.5 0.0 all-gather.2.cloned.1.call-start
  6.5 0.7 convert_multiply_fusion
  7.2 4.8 broadcast_multiply_fusion
  12.0 0.0 all-gather.2.cloned.1.call-update
  12.0 52.6 %all_to_all.37 = f32[4,64,4096]{2,1,0:T(8,128)S(1)} all-to-all(f32[4,64,4096]{2,1,0:T(8,128)} %bitcast.17), channel_id=1, replica_groups=mesh['row'=8,'col'=4] {'col'}, dimensions={0} | all-to-all | bytes 8388608 | tf_op jit(solution)/shard_map/all_to_all | solution.py:21
  64.7 4.8 copy.13
  69.4 5.5 all_to_all.30
  74.9 4.6 copy.14
  79.5 136.8 %all_to_all.38 = f32[64,8,2048]{2,0,1:T(8,128)S(1)} all-to-all(f32[64,8,2048]{2,0,1:T(8,128)S(1)} %copy.14), channel_id=1, replica_groups=mesh['row'=8,'col'=4] {'row'}, dimensions={1} | all-to-all | bytes 8388608 | tf_op jit(solution)/shard_map/all_to_all | solution.py:22
  216.3 8.3 stack.10
  224.6 7.3 all-to-all-start.2
  231.9 465.6 %all-gather.2.cloned.1.call-done = f32[2048,4096]{1,0:T(8,128)} async-done(((f32[256,4096]{1,0:T(8,128)}), f32[2048,4096]{1,0:T(8,128)}) %all-gather.2.cloned.1.call-update) | async-done | bytes 33554448 | tf_op jit(solution)/shard_map/all_gather | solution.py:20
  697.5 23.1 %copy.12 = f32[4,8,64,4096]{3,2,1,0:T(8,128)} copy(f32[4,8,64,4096]{3,2,0,1:T(8,128)} %bitcast.14) | data formatting | bytes 67108864 | tf_op jit(solution)/shard_map/transpose | solution.py:29
  720.6 0.0 all-to-all-done.2
  720.6 222.4 %convolution_bitcast_fusion = f32[2048,4096]{0,1:T(8,128)} fusion(f32[2048,4096]{1,0:T(8,128)} %bitcast.15, f32[2048,2048]{1,0:T(8,128)} %bitcast.7), kind=kOutput, calls=%fused_computation | convolution fusion | flops 206158430208 | bytes 83886080 | tf_op jit(solution)/shard_map/dot_general | solution.py:8
  943.0 31.1 %copy.15 = f32[2048,4096]{1,0:T(8,128)} copy(f32[2048,4096]{0,1:T(8,128)} %convolution_bitcast_fusion) | data formatting | bytes 67108864 | tf_op jit(solution)/shard_map/dot_general | solution.py:8
Async XLA Ops:
  6.5 691.0 %all-gather.2.cloned.1.call-start = ((), (), s32[]{:S(2)}) async-start(), calls=%async_computation.3 | async-start | bytes 37748736 | tf_op jit(solution)/shard_map/all_gather | solution.py:20
  224.6 496.0 %all-to-all-start.2 = ((f32[4,512,2048]{2,1,0:T(8,128)}), f32[4,512,2048]{2,1,0:T(8,128)}, u32[]{:S(2)}, u32[]{:S(2)}) async-start(f32[4,512,2048]{2,1,0:T(8,128)} %stack.10), calls=%async_computation.2 | async-start | bytes 33554432 | tf_op jit(solution)/shard_map/all_to_all | solution.py:34
Sparse Core Ops, SparseCore 0:
  12.2 685.3 all-gather.1
